TPU v7x, 512 devices: a whole 4x8x8 slice. The times are simulated.
512 devices in a mesh: orb: 32 (over x, y), grid: 16 (over z, core).
Axes of the slice: x: 4, y: 8, z: 8, core: 2. Of those that a mesh axis runs over, the one named last changes fastest.
Arguments:
- orbitals: float32 [128, 32, 4096], P('orb', 'grid'), may hold values from -6 to 6
- rotation: float32 [128, 128], replicated, may hold values from -0.5 to 0.5
- tile_list: int32 [64, 2], replicated, may hold values from 0 to 31, as said below
- pair_mask: int32 [128, 128], replicated, may hold values from 0 to 1, as said below
Outputs:
- exchange_term: float32 [128, 32, 4096], P('orb', 'grid')
Inputs may be any that keep to these rules, and one draw needn't show every extreme that they name: `tile_list`: row t names one tile: its target block and its source block of 4 orbitals each; no tile is named twice. `pair_mask`: among the 1024 orbital pairs that lie in listed tiles, exactly 512 are 1.
All inputs are finite; a program needn't handle non-finite values.
Results may differ from a plain program's by a relative error of at most 0.0003.
Values sent between devices are 32-bit elements; how exact they have to be, the bound alone decides.
A program may use at most 64 MiB of HBM per device.

v0:
```python
import jax
import jax.numpy as jnp
from jax import lax
from jax.sharding import PartitionSpec as P

NORB = 128
BLK = 4
NX = 32
NY = 64
NZ = 64
LIVE_DEV = 1
precise = lax.Precision.HIGHEST
coupling = 0.25
screening = 0.1


def split_up(array, dim, devices):
    dims = array.shape
    tiles = array.reshape(*dims[:dim], devices, dims[dim] // devices, *dims[dim + 1 :])
    return jnp.moveaxis(tiles, dim, 0)


def laid_out(tiles, dim):
    dims = list(tiles.shape[1:])
    dims[dim] *= tiles.shape[0]
    return jnp.moveaxis(tiles, 0, dim).reshape(dims)


def joined_exchange(array, axis, axes, splits, concats):
    sizes = [lax.axis_size(a) for a in axes]
    tiles = split_up(array, splits[0], sizes[0])
    tiles = jnp.moveaxis(split_up(tiles, splits[1] + 1, sizes[1]), 0, 1)
    inside = tiles.shape[2:]
    tiles = tiles.reshape(-1, *inside)
    tiles = lax.all_to_all(tiles, axis, split_axis=0, concat_axis=0, tiled=True)
    tiles = laid_out(tiles.reshape(*sizes, *inside), concats[0] + 1)
    return laid_out(tiles, concats[1])


def sine_table(length):
    wave_index = jnp.arange(length, dtype=jnp.float32) + 1.0
    return jnp.sqrt(2.0 / (length + 1.0)) * jnp.sin(
        jnp.pi * wave_index[:, None] * wave_index[None, :] / (length + 1.0)
    )


def eigen_values(length):
    wave_index = jnp.arange(length, dtype=jnp.float32) + 1.0
    return 2.0 - 2.0 * jnp.cos(jnp.pi * wave_index / (length + 1.0))


def green_kernel(size_x, size_y, size_z):
    summed = (
        eigen_values(size_x)[:, None, None]
        + eigen_values(size_y)[None, :, None]
        + eigen_values(size_z)[None, None, :]
    )
    return coupling / (summed + screening)


def pair_lists(tile_list, pair_mask):
    within = jnp.arange(BLK * BLK, dtype=jnp.int32)
    targets = (BLK * tile_list[:, 0:1] + within[None, :] // BLK).reshape(-1)
    sources = (BLK * tile_list[:, 1:2] + within[None, :] % BLK).reshape(-1)
    return (targets, sources, pair_mask[targets, sources])


def compact(targets, sources, live_flags, number):
    ranking = jnp.cumsum(live_flags) - 1
    places = jnp.where(live_flags == 1, ranking, number)
    picked = (
        jnp.zeros((number,), jnp.int32)
        .at[places]
        .set(jnp.arange(live_flags.shape[0], dtype=jnp.int32), mode="drop")
    )
    return (targets[picked], sources[picked])


def along_z(values, matrix):
    number, planes, width_yz = values.shape
    size_z = matrix.shape[0]
    shaped = values.reshape(number, planes, width_yz // size_z, size_z)
    return jnp.einsum("pxrz,zk->pxrk", shaped, matrix, precision=precise).reshape(
        number, planes, width_yz
    )


def along_y(values, matrix):
    number, planes, width_yz = values.shape
    size_y = matrix.shape[0]
    shaped = values.reshape(number, planes, size_y, width_yz // size_y)
    return jnp.einsum("pxyz,yk->pxkz", shaped, matrix, precision=precise).reshape(
        number, planes, width_yz
    )


def along_x(values, matrix):
    return jnp.einsum("pxc,xk->pkc", values, matrix, precision=precise)


def regroup(values, outer, middle):
    return values.reshape(outer, middle, -1).transpose(1, 0, 2).reshape(-1)


def on_device(orbitals, rotation, tile_list, pair_mask):
    rotated = jnp.einsum(
        "ij,ixc->jxc",
        rotation,
        lax.all_to_all(orbitals, "orb", split_axis=2, concat_axis=0, tiled=True),
        precision=precise,
    )
    planes = rotated.shape[1]
    width_yz = rotated.shape[2]
    targets, sources, live_flags = pair_lists(tile_list, pair_mask)
    weights = live_flags.astype(jnp.float32)
    matrix_x = sine_table(NX)
    matrix_y = sine_table(NY)
    matrix_z = sine_table(NZ)
    kernel = green_kernel(NX, NY, NZ).reshape(NX, NY * NZ)
    orbital_ids = jnp.arange(NORB, dtype=jnp.int32)
    targets, sources = compact(
        targets, sources, live_flags, LIVE_DEV * lax.axis_size("orb") * lax.axis_size("grid")
    )
    density = rotated[targets] * rotated[sources]
    number = density.shape[0]
    spectrum = along_z(density, matrix_z)
    spectrum = joined_exchange(spectrum, ("orb", "grid"), ("orb", "grid"), (0, 0), (2, 1))
    spectrum = along_x(along_y(spectrum, matrix_y), matrix_x) * kernel
    spectrum = along_y(along_x(spectrum, matrix_x), matrix_y)
    spectrum = joined_exchange(spectrum, ("orb", "grid"), ("orb", "grid"), (2, 1), (0, 0))
    outer = lax.axis_size("orb")
    middle = lax.axis_size("grid")
    targets = regroup(targets, outer, middle)
    sources = regroup(sources, outer, middle)
    weights = regroup(weights, outer, middle)
    potential = along_z(spectrum, matrix_z)
    products = potential * rotated[sources]
    selector = (targets[None, :] == orbital_ids[:, None]).astype(jnp.float32)
    partial_value = -jnp.dot(
        selector, products.reshape(number, planes * width_yz), precision=precise
    )
    partial_value = partial_value.reshape(NORB, planes, width_yz)
    return lax.all_to_all(partial_value, "orb", split_axis=0, concat_axis=2, tiled=True)


def solution(mesh):
    in_specs = (P("orb", "grid", None), P(), P(), P())
    out_specs = P("orb", "grid", None)
    return jax.shard_map(
        on_device, mesh=mesh, in_specs=in_specs, out_specs=out_specs, check_vma=False
    )
```

profile of v0, /device:TPU:8, one launch (start us, length us, event | category | flops | bytes accessed | tf_op | source)
XLA Modules:
  0.0 161.6 jit_solution(12426053909212209676)
XLA Ops:
  0.0 5.4 %copy.48 = f32[4,2,4096]{0,1,2:T(2,128)} copy(f32[4,2,4096]{2,1,0:T(2,128)} %param.4) | data formatting | bytes 262144 | tf_op args[0]
  5.4 8.6 %reshape.432 = f32[32,1,1024]{2,1,0:T(1,128)} reshape(f32[4096,2,4]{2,1,0:T(2,128)} %bitcast.97) | data formatting | bytes 262144
  14.0 10.2 %all-to-all-start = ((f32[32,1,1024]{2,1,0:T(1,128)}), f32[32,1,1024]{2,1,0:T(1,128)S(1)}, u32[]{:S(2)}, u32[]{:S(2)}) async-start(f32[32,1,1024]{2,1,0:T(1,128)} %reshape.432), calls=%async_computation | async-start | bytes 262144 | tf_op jit(solution)/shard_map/all_to_all | solution.py:109
  24.6 6.8 %gather_fusion = s32[1024]{0:T(1024)S(1)} fusion(s32[128,128]{1,0:T(8,128)S(1)} %copy-done.1, s32[1024]{0:T(1024)S(1)} %bitcast.95), kind=kCustom, calls=%fused_computation | custom fusion | bytes 16384 | tf_op jit(solution)/shard_map/gather | solution.py:65
  32.1 4.3 %scatter_custom_fusion = s32[512]{0:T(512)S(1)} fusion(s32[1024]{0:T(1024)S(1)} %bitcast.114, s32[1024]{0:T(1024)S(1)} %iota.52, s32[]{:T(128)} %constant.64.clone.1), kind=kCustom, calls=%fused_computation.80 | custom fusion | bytes 2052 | tf_op jit(solution)/shard_map/scatter | solution.py:74
  36.4 2.3 %gather_fusion.3 = s32[512]{0:T(512)S(1)} fusion(s32[1024]{0:T(1024)S(1)} %add.263, s32[1024]{0:T(1024)S(1)} %pad_clamp_fusion.3), kind=kCustom, calls=%fused_computation.3 | custom fusion | bytes 6144 | tf_op jit(solution)/shard_map/gather | solution.py:76
  38.7 2.3 %gather_fusion.1 = s32[512]{0:T(512)S(1)} fusion(s32[1024]{0:T(1024)S(1)} %add.248, s32[1024]{0:T(1024)S(1)} %pad_clamp_fusion.3), kind=kCustom, calls=%fused_computation.1 | custom fusion | bytes 6144 | tf_op jit(solution)/shard_map/gather | solution.py:76
  41.6 0.9 reduce.2
  42.5 7.8 %reshape.433 = f32[4096,2,4]{2,1,0:T(2,128)} reshape(f32[32,1024]{1,0:T(8,128)S(1)} %reduce.2) | data formatting | bytes 262144
  50.3 5.2 %copy.49 = f32[4,2,32,128]{3,0,2,1:T(4,128)S(1)} copy(f32[4,2,32,128]{0,1,3,2:T(2,128)} %bitcast.96) | data formatting | bytes 262144 | tf_op jit(solution)/shard_map/all_to_all | solution.py:109
  55.9 2.1 %gather_fusion.2 = f32[512,2,128]{2,1,0:T(2,128)S(1)} fusion(f32[128,2,128]{2,1,0:T(2,128)S(1)} %copy.51, s32[1024]{0:T(1024)S(1)} %pad_clamp_fusion.2), kind=kCustom, calls=%fused_computation.2 | custom fusion | bytes 1050624 | tf_op jit(solution)/shard_map/gather | solution.py:124
  58.0 2.1 %gather_fusion.4 = f32[512,2,128]{2,1,0:T(2,128)S(1)} fusion(f32[128,2,128]{2,1,0:T(2,128)S(1)} %copy.51, s32[1024]{0:T(1024)S(1)} %pad_clamp_fusion.1), kind=kCustom, calls=%fused_computation.4 | custom fusion | bytes 1050624 | tf_op jit(solution)/shard_map/gather | solution.py:124
  61.4 1.0 copy.54
  62.4 20.7 %all-to-all-start.1 = ((f32[512,1,2,128]{3,2,1,0:T(2,128)}), f32[512,1,2,128]{3,2,1,0:T(2,128)S(1)}, u32[]{:S(2)}, u32[]{:S(2)}) async-start(f32[512,1,2,128]{3,2,1,0:T(2,128)} %copy.54), calls=%async_computation.1 | async-start | bytes 1048576 | tf_op jit(solution)/shard_map/all_to_all | solution.py:35
  84.1 20.1 %all-to-all-done.1 = f32[512,1,2,128]{3,2,1,0:T(2,128)S(1)} async-done(((f32[512,1,2,128]{3,2,1,0:T(2,128)}), f32[512,1,2,128]{3,2,1,0:T(2,128)S(1)}, u32[]{:S(2)}, u32[]{:S(2)}) %all-to-all-start.1) | async-done | bytes 524320 | tf_op jit(solution)/shard_map/all_to_all | solution.py:35
  104.6 1.2 convolution_bitcast_fusion.1
  107.3 1.7 %fusion.4 = f32[32,64,64]{2,0,1:T(8,128)S(1)} fusion(f32[64,64,32]{1,0,2:T(8,128)S(1)} %dot_general.38, f32[32]{0:T(128)S(1)} %get-tuple-element.11, f32[32]{0:T(128)S(1)} %get-tuple-element.12), kind=kOutput, calls=%fused_computation.15 | convolution fusion | flops 50334720 | bytes 1048832 | tf_op jit(solution)/shard_map/pxc,xk->pkc/dot_general | solution.py:98
  109.0 1.8 %convolution_bitcast_fusion = f32[1,32,64,64]{3,2,1,0:T(8,128)S(1)} fusion(f32[32,64,64]{2,0,1:T(8,128)S(1)} %fusion.4, f32[64]{0:T(128)S(1)} %get-tuple-element.9, f32[64]{0:T(128)S(1)} %get-tuple-element.10), kind=kOutput, calls=%fused_computation.9 | convolution fusion | flops 100675584 | bytes 1049088 | tf_op jit(solution)/shard_map/pxyz,yk->pxkz/dot_general | solution.py:92
  111.0 1.1 copy.59
  112.1 9.7 %all-to-all-start.2 = ((f32[512,1,2,128]{3,2,1,0:T(2,128)}), f32[512,1,2,128]{3,2,1,0:T(2,128)S(1)}, u32[]{:S(2)}, u32[]{:S(2)}) async-start(f32[512,1,2,128]{3,2,1,0:T(2,128)} %bitcast.30), calls=%async_computation.2 | async-start | bytes 1048576 | tf_op jit(solution)/shard_map/all_to_all | solution.py:35
  122.3 2.1 %gather_fusion.5 = f32[512,2,128]{2,1,0:T(2,128)S(1)} fusion(f32[128,2,128]{2,1,0:T(2,128)S(1)} %copy.51, s32[1024]{0:T(1024)S(1)} %pad_clamp_fusion), kind=kCustom, calls=%fused_computation.5 | custom fusion | bytes 1050624 | tf_op jit(solution)/shard_map/gather | solution.py:137
  124.6 18.3 %all-to-all-done.2 = f32[512,1,2,128]{3,2,1,0:T(2,128)S(1)} async-done(((f32[512,1,2,128]{3,2,1,0:T(2,128)}), f32[512,1,2,128]{3,2,1,0:T(2,128)S(1)}, u32[]{:S(2)}, u32[]{:S(2)}) %all-to-all-start.2) | async-done | bytes 524320 | tf_op jit(solution)/shard_map/all_to_all | solution.py:35
  143.8 1.5 fusion.1
  145.8 15.0 %all_to_all.46 = f32[128,2,128]{2,1,0:T(2,128)S(1)} all-to-all(f32[128,2,128]{2,1,0:T(2,128)S(1)} %reshape.368), channel_id=1, replica_groups=mesh['orb'=32,'grid'=16] {'orb'}, dimensions={0} | all-to-all | bytes 262144 | tf_op jit(solution)/shard_map/all_to_all | solution.py:143
  (69 shorter events, 9.2 us)
Async XLA Ops:
  0.0 55.5 %copy-start = (f32[128,128]{1,0:T(8,128)S(1)}, f32[128,128]{1,0:T(8,128)}, u32[]{:S(2)}) copy-start(f32[128,128]{1,0:T(8,128)} %param.5) | copy-start | bytes 196612
  0.0 24.2 %copy-start.2 = (s32[64,2]{0,1:T(2,128)S(1)}, s32[64,2]{0,1:T(2,128)}, u32[]{:S(2)}) copy-start(s32[64,2]{0,1:T(2,128)} %param.6) | copy-start | bytes 1540
  0.0 24.6 %copy-start.1 = (s32[128,128]{1,0:T(8,128)S(1)}, s32[128,128]{1,0:T(8,128)}, u32[]{:S(2)}) copy-start(s32[128,128]{1,0:T(8,128)} %param.7) | copy-start | bytes 196612
  14.0 27.1 %all-to-all-start = ((f32[32,1,1024]{2,1,0:T(1,128)}), f32[32,1,1024]{2,1,0:T(1,128)S(1)}, u32[]{:S(2)}, u32[]{:S(2)}) async-start(f32[32,1,1024]{2,1,0:T(1,128)} %reshape.432), calls=%async_computation | async-start | bytes 262144 | tf_op jit(solution)/shard_map/all_to_all | solution.py:109
  62.4 41.8 %all-to-all-start.1 = ((f32[512,1,2,128]{3,2,1,0:T(2,128)}), f32[512,1,2,128]{3,2,1,0:T(2,128)S(1)}, u32[]{:S(2)}, u32[]{:S(2)}) async-start(f32[512,1,2,128]{3,2,1,0:T(2,128)} %copy.54), calls=%async_computation.1 | async-start | bytes 1048576 | tf_op jit(solution)/shard_map/all_to_all | solution.py:35
  112.1 30.9 %all-to-all-start.2 = ((f32[512,1,2,128]{3,2,1,0:T(2,128)}), f32[512,1,2,128]{3,2,1,0:T(2,128)S(1)}, u32[]{:S(2)}, u32[]{:S(2)}) async-start(f32[512,1,2,128]{3,2,1,0:T(2,128)} %bitcast.30), calls=%async_computation.2 | async-start | bytes 1048576 | tf_op jit(solution)/shard_map/all_to_all | solution.py:35
where the time goes:
time: 162 us
  local copies, waits for them, and re-layouts  56.7 us (35%)
  starting transfers between devices  40.6 us (25%)
  waiting for transfers between devices  38.4 us (24%)
  blocking collectives  15 us (9%)
  matrix products  8.41 us (5%)
  other arithmetic  2.05 us (1%)
    all_to_all x2, waiting for transfers between devices, joined_exchange(): tiles = lax.all_to_all(tiles, axis, split_axis=0, concat_axis=0, tiled=True)  38.4 us
    all_to_all x2, starting transfers between devices, joined_exchange(): tiles = lax.all_to_all(tiles, axis, split_axis=0, concat_axis=0, tiled=True)  30.5 us
    unnamed x9, local copies, waits for them, and re-layouts  21.8 us
    all_to_all x1, blocking collectives, on_device(): lax.all_to_all(partial_value, 'orb', split_axis=0, concat_axis=2, tiled=T...  15 us
    all_to_all x1, starting transfers between devices, on_device(): lax.all_to_all(orbitals, 'orb', split_axis=2, concat_axis=0, tiled=True)  10.2 us
    gather x1, local copies, waits for them, and re-layouts, pair_lists(): return (targets, sources, pair_mask[targets, sources])  6.8 us
    all_to_all x2, local copies, waits for them, and re-layouts, on_device(): lax.all_to_all(orbitals, 'orb', split_axis=2, concat_axis=0, tiled=True)  5.67 us
    gather x2, local copies, waits for them, and re-layouts, compact(): return (targets[picked], sources[picked])  4.58 us
  transfers between devices with their start and end apart: 3, of which 2 were waited for; matrix products, arithmetic and copies ran while one was open for 13% of the time, Pallas kernels for 0%

commit v1 on v0

--- a/solution.py
+++ b/solution.py
@@ -2,6 +2,7 @@
 import jax.numpy as jnp
 from jax import lax
 from jax.sharding import PartitionSpec as P
+from jax.lax import all_to_all, axis_size
 
 NORB = 128
 BLK = 4
@@ -12,6 +13,9 @@
 precise = lax.Precision.HIGHEST
 coupling = 0.25
 screening = 0.1
+name_axis_part = lambda inner_x: jnp.concatenate(
+    all_to_all(jnp.stack(jnp.split(inner_x, axis_size("orb"), axis=2)), "orb", 0, 0), axis=0
+)
 
 
 def split_up(array, dim, devices):
@@ -103,12 +107,7 @@
 
 
 def on_device(orbitals, rotation, tile_list, pair_mask):
-    rotated = jnp.einsum(
-        "ij,ixc->jxc",
-        rotation,
-        lax.all_to_all(orbitals, "orb", split_axis=2, concat_axis=0, tiled=True),
-        precision=precise,
-    )
+    rotated = jnp.einsum("ij,ixc->jxc", rotation, name_axis_part(orbitals), precision=precise)
     planes = rotated.shape[1]
     width_yz = rotated.shape[2]
     targets, sources, live_flags = pair_lists(tile_list, pair_mask)

time: 162 us -> 177 us (1.093)
  local copies, waits for them, and re-layouts: 56.7 us -> 71.5 us
    unnamed x9 -> x37, local copies, waits for them, and re-layouts: 21.8 us -> 41 us
    all_to_all x2 -> x0, local copies, waits for them, and re-layouts: 5.67 us -> none  [on_device(): lax.all_to_all(orbitals, 'orb', split_axis=2, concat_axis=0, tiled=True)]
  transfers between devices with their start and end apart: 3 -> 3, of which waited for: 2 -> 2; matrix products, arithmetic and copies ran while one was open for 13% -> 12% of each run, Pallas kernels for 0% -> 0%
where the time goes in v1:
time: 177 us; the launch traced here: 175 us
  local copies, waits for them, and re-layouts  71.5 us (40%)
  starting transfers between devices  40.5 us (23%)
  waiting for transfers between devices  38.3 us (22%)
  blocking collectives  15 us (8%)
  matrix products  8.49 us (5%)
    unnamed x37, local copies, waits for them, and re-layouts  41 us
    all_to_all x2, waiting for transfers between devices, joined_exchange(): tiles = lax.all_to_all(tiles, axis, split_axis=0, concat_axis=0, tiled=True)  38.3 us
    all_to_all x2, starting transfers between devices, joined_exchange(): tiles = lax.all_to_all(tiles, axis, split_axis=0, concat_axis=0, tiled=True)  30.3 us
    all_to_all x1, blocking collectives, on_device(): lax.all_to_all(partial_value, 'orb', split_axis=0, concat_axis=2, tiled=T...  15 us
    all_to_all x1, starting transfers between devices, all_to_all(jnp.stack(jnp.split(inner_x, axis_size('orb'), axis=2)), 'orb'...  10.2 us
    gather x1, local copies, waits for them, and re-layouts, pair_lists(): return (targets, sources, pair_mask[targets, sources])  6.79 us
    gather x2, local copies, waits for them, and re-layouts, compact(): return (targets[picked], sources[picked])  4.58 us
    scatter x1, local copies, waits for them, and re-layouts, compact(): picked = jnp.zeros((number,), jnp.int32).at[places].set(jnp.arange(live_f...  4.3 us
  transfers between devices with their start and end apart: 3, of which 2 were waited for; matrix products, arithmetic and copies ran while one was open for 12% of the time, Pallas kernels for 0%

profile of v1, /device:TPU:8, one launch (start us, length us, event | category | flops | bytes accessed | tf_op | source)
XLA Modules:
  0.0 175.3 jit_solution(1320229226145944315)
XLA Ops:
  0.0 1.3 constant_dynamic-update-slice_fusion.31
  3.9 1.3 constant_dynamic-update-slice_fusion.28
  7.7 1.3 constant_dynamic-update-slice_fusion.25
  11.6 1.3 constant_dynamic-update-slice_fusion.22
  15.4 1.3 constant_dynamic-update-slice_fusion.19
  30.7 1.3 constant_dynamic-update-slice_fusion.7
  32.0 1.3 constant_dynamic-update-slice_fusion.6
  33.3 1.3 constant_dynamic-update-slice_fusion.5
  41.0 10.2 %all-to-all-start = ((f32[32,4,2,128]{3,2,1,0:T(2,128)}), f32[32,4,2,128]{3,2,1,0:T(2,128)S(1)}, u32[]{:S(2)}, u32[]{:S(2)}) async-start(f32[32,4,2,128]{3,2,1,0:T(2,128)} %constant_dynamic-update-slice_fusion), calls=%async_computation | async-start | bytes 262144 | tf_op jit(solution)/shard_map/all_to_all | solution.py:17
  52.9 6.8 %gather_fusion = s32[1024]{0:T(1024)S(1)} fusion(s32[128,128]{1,0:T(8,128)S(1)} %copy-done.1, s32[1024]{0:T(1024)S(1)} %bitcast.155), kind=kCustom, calls=%fused_computation | custom fusion | bytes 16384 | tf_op jit(solution)/shard_map/gather | solution.py:69
  60.3 4.3 %scatter_custom_fusion = s32[512]{0:T(512)S(1)} fusion(s32[1024]{0:T(1024)S(1)} %bitcast.172, s32[1024]{0:T(1024)S(1)} %iota.52, s32[]{:T(128)} %constant.64.clone.1), kind=kCustom, calls=%fused_computation.113 | custom fusion | bytes 2052 | tf_op jit(solution)/shard_map/scatter | solution.py:78
  64.7 2.3 %gather_fusion.1 = s32[512]{0:T(512)S(1)} fusion(s32[1024]{0:T(1024)S(1)} %add.248, s32[1024]{0:T(1024)S(1)} %pad_clamp_fusion.3), kind=kCustom, calls=%fused_computation.1 | custom fusion | bytes 6144 | tf_op jit(solution)/shard_map/gather | solution.py:80
  67.0 2.3 %gather_fusion.3 = s32[512]{0:T(512)S(1)} fusion(s32[1024]{0:T(1024)S(1)} %add.263, s32[1024]{0:T(1024)S(1)} %pad_clamp_fusion.3), kind=kCustom, calls=%fused_computation.3 | custom fusion | bytes 6144 | tf_op jit(solution)/shard_map/gather | solution.py:80
  69.9 2.1 %gather_fusion.2 = f32[512,2,128]{2,1,0:T(2,128)S(1)} fusion(f32[128,2,128]{2,1,0:T(2,128)S(1)} %copy.45, s32[1024]{0:T(1024)S(1)} %pad_clamp_fusion.2), kind=kCustom, calls=%fused_computation.2 | custom fusion | bytes 1050624 | tf_op jit(solution)/shard_map/gather | solution.py:123
  72.0 2.1 %gather_fusion.4 = f32[512,2,128]{2,1,0:T(2,128)S(1)} fusion(f32[128,2,128]{2,1,0:T(2,128)S(1)} %copy.45, s32[1024]{0:T(1024)S(1)} %pad_clamp_fusion.1), kind=kCustom, calls=%fused_computation.4 | custom fusion | bytes 1050624 | tf_op jit(solution)/shard_map/gather | solution.py:123
  76.4 20.7 %all-to-all-start.1 = ((f32[512,1,2,128]{3,2,1,0:T(2,128)}), f32[512,1,2,128]{3,2,1,0:T(2,128)S(1)}, u32[]{:S(2)}, u32[]{:S(2)}) async-start(f32[512,1,2,128]{3,2,1,0:T(2,128)} %copy.48), calls=%async_computation.1 | async-start | bytes 1048576 | tf_op jit(solution)/shard_map/all_to_all | solution.py:39
  98.1 20.0 %all-to-all-done.1 = f32[512,1,2,128]{3,2,1,0:T(2,128)S(1)} async-done(((f32[512,1,2,128]{3,2,1,0:T(2,128)}), f32[512,1,2,128]{3,2,1,0:T(2,128)S(1)}, u32[]{:S(2)}, u32[]{:S(2)}) %all-to-all-start.1) | async-done | bytes 524320 | tf_op jit(solution)/shard_map/all_to_all | solution.py:39
  121.3 1.7 fusion.4
  122.9 1.8 %convolution_bitcast_fusion = f32[1,32,64,64]{3,2,1,0:T(8,128)S(1)} fusion(f32[32,64,64]{2,0,1:T(8,128)S(1)} %fusion.4, f32[64]{0:T(128)S(1)} %get-tuple-element.9, f32[64]{0:T(128)S(1)} %get-tuple-element.10), kind=kOutput, calls=%fused_computation.9 | convolution fusion | flops 100675584 | bytes 1049088 | tf_op jit(solution)/shard_map/pxyz,yk->pxkz/dot_general | solution.py:96
  126.0 9.6 %all-to-all-start.2 = ((f32[512,1,2,128]{3,2,1,0:T(2,128)}), f32[512,1,2,128]{3,2,1,0:T(2,128)S(1)}, u32[]{:S(2)}, u32[]{:S(2)}) async-start(f32[512,1,2,128]{3,2,1,0:T(2,128)} %bitcast.61), calls=%async_computation.2 | async-start | bytes 1048576 | tf_op jit(solution)/shard_map/all_to_all | solution.py:39
  136.1 2.1 %gather_fusion.5 = f32[512,2,128]{2,1,0:T(2,128)S(1)} fusion(f32[128,2,128]{2,1,0:T(2,128)S(1)} %copy.45, s32[1024]{0:T(1024)S(1)} %pad_clamp_fusion), kind=kCustom, calls=%fused_computation.5 | custom fusion | bytes 1050624 | tf_op jit(solution)/shard_map/gather | solution.py:136
  138.4 18.3 %all-to-all-done.2 = f32[512,1,2,128]{3,2,1,0:T(2,128)S(1)} async-done(((f32[512,1,2,128]{3,2,1,0:T(2,128)}), f32[512,1,2,128]{3,2,1,0:T(2,128)S(1)}, u32[]{:S(2)}, u32[]{:S(2)}) %all-to-all-start.2) | async-done | bytes 524320 | tf_op jit(solution)/shard_map/all_to_all | solution.py:39
  157.5 1.5 fusion.1
  159.6 15.0 %all_to_all.33 = f32[128,2,128]{2,1,0:T(2,128)S(1)} all-to-all(f32[128,2,128]{2,1,0:T(2,128)S(1)} %reshape.372), channel_id=1, replica_groups=mesh['orb'=32,'grid'=16] {'orb'}, dimensions={0} | all-to-all | bytes 262144 | tf_op jit(solution)/shard_map/all_to_all | solution.py:142
  (95 shorter events, 44.0 us)
Async XLA Ops:
  0.0 69.3 %copy-start = (f32[128,128]{1,0:T(8,128)S(1)}, f32[128,128]{1,0:T(8,128)}, u32[]{:S(2)}) copy-start(f32[128,128]{1,0:T(8,128)} %param.5) | copy-start | bytes 196612
  41.0 28.3 %all-to-all-start = ((f32[32,4,2,128]{3,2,1,0:T(2,128)}), f32[32,4,2,128]{3,2,1,0:T(2,128)S(1)}, u32[]{:S(2)}, u32[]{:S(2)}) async-start(f32[32,4,2,128]{3,2,1,0:T(2,128)} %constant_dynamic-update-slice_fusion), calls=%async_computation | async-start | bytes 262144 | tf_op jit(solution)/shard_map/all_to_all | solution.py:17
  51.2 0.7 copy-start.2
  52.1 0.8 copy-start.1
  76.4 41.8 %all-to-all-start.1 = ((f32[512,1,2,128]{3,2,1,0:T(2,128)}), f32[512,1,2,128]{3,2,1,0:T(2,128)S(1)}, u32[]{:S(2)}, u32[]{:S(2)}) async-start(f32[512,1,2,128]{3,2,1,0:T(2,128)} %copy.48), calls=%async_computation.1 | async-start | bytes 1048576 | tf_op jit(solution)/shard_map/all_to_all | solution.py:39
  126.0 30.6 %all-to-all-start.2 = ((f32[512,1,2,128]{3,2,1,0:T(2,128)}), f32[512,1,2,128]{3,2,1,0:T(2,128)S(1)}, u32[]{:S(2)}, u32[]{:S(2)}) async-start(f32[512,1,2,128]{3,2,1,0:T(2,128)} %bitcast.61), calls=%async_computation.2 | async-start | bytes 1048576 | tf_op jit(solution)/shard_map/all_to_all | solution.py:39
